TPU v7x, 32 devices: a whole 2x2x4 slice. The times are simulated.
32 devices in a mesh: row: 8 (over z, core), col: 4 (over y, x).
Axes of the slice: x: 2, y: 2, z: 4, core: 2. Of those that a mesh axis runs over, the one named last changes fastest.
Arguments:
- flow_tiles: bfloat16 [8, 8, 256, 256], P('row', 'col'), may hold values from 0.1 to 25
- tile_cols: int32 [8, 8], P('row', 'col'), may hold values from -1 to 7, as said below
- pairs: int32 [512, 2], P(('row', 'col')), may hold values from -1 to 7, as said below
Outputs:
- new_flow: float32 [8, 8, 256, 256], P('row', 'col')
Inputs may be any that keep to these rules, and one draw needn't show every extreme that they name: `tile_cols`: the stored slots of device (r, c) have distinct tile columns, each congruent to c modulo the col axis's size; tile row r stores tile column r. `pairs`: device (r, c) lists, in some order and without repeats, exactly the (k, s) for which slot s of the device is stored and M[r, k] and M[k, tile_cols[r, c * 2 + s]] are both stored tiles; its other rows are (-1, -1). Some device uses all 16 rows.
All inputs are finite; a program needn't handle non-finite values.
Results may differ from a plain program's by a relative error of at most 0.0003.
Values may be sent and summed in bfloat16 or wider, within the bound.
A program may use at most 64 MiB of HBM per device.

v0:
```python
import functools
import math

import jax
import jax.numpy as jnp
from jax import lax
from jax.experimental import pallas as pl
from jax.experimental.pallas import tpu as pltpu
from jax.sharding import PartitionSpec as P

MESH = pl.DeviceIdType.MESH
CORES = 2
SPLIT = 2


def remote(src, dst, send_sem, recv_sem, device):
    return pltpu.make_async_remote_copy(
        src_ref=src,
        dst_ref=dst,
        send_sem=send_sem,
        recv_sem=recv_sem,
        device_id=device,
        device_id_type=MESH,
    )


def kernel(
    nrow, ncol, cols_hbm, flow_hbm, out_ref,
    cols, raw, own, blocks, left, acc, swap, result, flags, sums,
    in_sem, up_send, dn_send, mate_send, recv, left_send, left_recv,
    left_mate, flag_sem, swap_sem, sum_send, sum_recv,
):
    tiles, width = raw.shape[0], raw.shape[2]
    depth = own.shape[1]
    share = tiles // CORES
    pieces = share * SPLIT
    planes = nrow // CORES
    row, col = lax.axis_index("row"), lax.axis_index("col")
    z, core = row // CORES, row % CORES
    mate = (row + 1 - 2 * core, col)
    mate_row = row + 1 - 2 * core
    above, below = (row + CORES, col), (row - CORES, col)
    has_above, has_below = z < planes - 1, z > 0
    ny = math.isqrt(ncol)
    ny = ny if ny * ny == ncol else 1
    nx = ncol // ny
    y, x = col // nx, col % nx
    half = tiles // 2

    def at(dy, dx):
        return ((y + dy) % ny) * nx + (x + dx) % nx

    along_x = [(0, dx) for dx in range(1, nx)]
    along_y = [(dy, 0) for dy in range(1, ny)]
    across = [(dy, dx) for dy, _ in along_y for _, dx in along_x]

    load_cols = pltpu.make_async_copy(cols_hbm, cols, in_sem.at[0])
    load_flow = pltpu.make_async_copy(flow_hbm.at[0], raw, in_sem.at[1])
    load_cols.start()
    load_flow.start()

    barrier = pltpu.get_barrier_semaphore()

    def greet(device):
        pl.semaphore_signal(barrier, inc=1, device_id=device, device_id_type=MESH)

    greet(mate)
    for d in along_x + along_y:
        greet((row, at(*d)))

    @pl.when(has_above)
    def _():
        for c in range(CORES):
            greet(((z + 1) * CORES + c, col))

    @pl.when(has_below)
    def _():
        for c in range(CORES):
            greet(((z - 1) * CORES + c, col))

    load_cols.wait()
    load_flow.wait()
    for t in range(tiles):
        target = col + ncol * t
        tile = jnp.zeros((width, width), jnp.float32)
        weight = jnp.float32(0)
        for s in range(tiles):
            w = (cols[0, s] == target).astype(jnp.float32)
            weight = weight + w
            tile = tile + raw[s].astype(jnp.float32) * w
        flags[core, t] = jnp.full((width,), weight, jnp.float32)
        tile = tile.astype(jnp.bfloat16)
        own[t * SPLIT:(t + 1) * SPLIT] = tile.reshape(SPLIT, depth, width)
        left[col, t, core] = tile
    blocks[row] = own[pl.ds(core * pieces, pieces)]

    ends = jnp.where(has_above, 1, 0) + jnp.where(has_below, 1, 0)
    pl.semaphore_wait(barrier, nx + ny - 1 + CORES * ends)

    def piece(src, k, u, send_sem, device):
        return remote(src, blocks.at[k, u], send_sem, recv.at[k, u], device)

    def arrived(k, u):
        piece(own.at[u], k, u, mate_send.at[u], mate).wait_recv()

    def to_mate(u):
        return piece(own.at[(1 - core) * pieces + u], row, u, mate_send.at[u], mate)

    def left_copy(c, t, rc, device, send_sem):
        part = left.at[c, t, rc]
        return remote(part, part, send_sem, left_recv.at[rc, c, t], device)

    def left_out(source, move, t):
        slot = (source[0] + move[0]) * nx + source[1] + move[1]
        return left_copy(at(*source), t, core, (row, at(*move)), left_send.at[slot, t])

    def left_to_mate(source, t):
        c = at(*source)
        return left_copy(c, t, core, mate, left_mate.at[c, t])

    def left_arrived(source, t):
        left_to_mate(source, t).wait_recv()
        left_to_mate(source, t).start()

    def left_relay():
        for t in range(half):
            for d in along_x:
                left_arrived(d, t)
                for move in along_y:
                    left_out(d, move, t).start()
        for t in range(half, tiles):
            for d in along_y:
                left_arrived(d, t)
                for move in along_x:
                    left_out(d, move, t).start()

    flag_copy = remote(flags.at[core], flags.at[core], flag_sem.at[0], flag_sem.at[1], mate)

    for u in range(pieces):
        for c in range(CORES):

            @pl.when(has_above)
            def _():
                piece(
                    own.at[c * pieces + u], row, u, up_send.at[0, c * pieces + u],
                    ((z + 1) * CORES + c, col),
                ).start()

            @pl.when(has_below)
            def _():
                piece(
                    own.at[c * pieces + u], row, u, dn_send.at[0, c * pieces + u],
                    ((z - 1) * CORES + c, col),
                ).start()

        if u == 0:
            for t in range(tiles):
                for d in along_x:
                    left_out((0, 0), d, t).start()
                for d in along_y:
                    left_out((0, 0), d, tiles - 1 - t).start()
    for u in range(pieces):
        to_mate(u).start()
    for t in range(tiles):
        left_to_mate((0, 0), t).start()
    flag_copy.start()

    acc[...] = jnp.zeros_like(acc)

    def relay(step):
        for c in range(CORES):
            if step == 1 and c == CORES - 1:
                left_relay()
            for u in range(pieces):

                @pl.when(z >= step)
                def _():
                    k = (z - step) * CORES + c
                    arrived(k, u)

                    @pl.when(has_above)
                    def _():
                        piece(
                            blocks.at[k, u], k, u, up_send.at[step, c * pieces + u], above
                        ).start()

                @pl.when(z + step < planes)
                def _():
                    k = (z + step) * CORES + c
                    arrived(k, u)

                    @pl.when(has_below)
                    def _():
                        piece(
                            blocks.at[k, u], k, u, dn_send.at[step, c * pieces + u], below
                        ).start()

    def multiply(k):
        a = left[k % ncol, k // ncol].reshape(CORES * width, width)
        for i in range(share):
            b = blocks[k, pl.ds(i * SPLIT, SPLIT)].reshape(width, width)
            c = jnp.dot(a, b, preferred_element_type=jnp.float32)
            acc[i] += c.reshape(CORES, width, width)

    def multiply_piece(k, u):
        h = u % SPLIT
        a = left[k % ncol, k // ncol, :, :, pl.ds(h * depth, depth)]
        c = jnp.dot(
            a.reshape(CORES * width, depth), blocks[k, u], preferred_element_type=jnp.float32
        )
        acc[u // SPLIT] += c.reshape(CORES, width, width)

    def compute(distance):
        for sign in (-1, 1) if distance else (1,):
            plane = z + sign * distance

            @pl.when((plane >= 0) & (plane < planes))
            def _():
                if distance == 0:
                    for u in range(pieces):
                        arrived(mate_row, u)
                for c in range(CORES):
                    multiply(plane * CORES + c)

    def last(distance):
        for sign in (-1, 1):
            plane = z + sign * distance

            @pl.when((plane >= 0) & (plane < planes))
            def _():
                for c in range(CORES):
                    for u in range(pieces):
                        k = plane * CORES + c
                        arrived(k, u)
                        multiply_piece(k, u)

    done = 0

    def catch_up(upto):
        nonlocal done
        if done == 0:
            for d in across:
                for t in range(tiles):
                    left_arrived(d, t)
            for c in range(ncol):
                for t in range(tiles):
                    left_copy(c, t, 1 - core, mate, left_mate.at[c, t]).wait_recv()
        while done < upto:
            compute(done)
            done += 1

    for step in range(1, planes - 1):
        if step > 2:
            catch_up(step)
        relay(step)
        if step == 1:
            for t in range(half, tiles):
                for d in along_x:
                    left_arrived(d, t)
            for t in range(half):
                for d in along_y:
                    left_arrived(d, t)
    catch_up(planes - 1)
    last(planes - 1)
    flag_copy.wait_recv()

    for i in range(share):
        t = core * share + i
        part = jnp.zeros((width,), jnp.float32)
        for c in range(CORES):
            part = part + jnp.sum(acc[i, c] * acc[i, c], axis=0) * flags[c, t]
        sums[row, i] = part

    def to_row(d):
        return remote(
            sums.at[row], sums.at[row], sum_send.at[d], sum_recv.at[row],
            ((row + d) % nrow, col),
        )

    for d in range(1, nrow):
        to_row(d).start()

    for i in range(share):
        other = acc[i, 1 - core]
        swap[i] = other * other
    swap_copy = remote(
        swap, result.at[pl.ds(core * share, share)], swap_sem.at[0], swap_sem.at[1], mate
    )
    swap_copy.start()
    for i in range(share):
        mine = acc[i, core]
        result[core * share + i] = mine * mine
    swap_copy.wait_recv()

    for d in range(1, nrow):
        other = (row + d) % nrow
        remote(
            sums.at[other], sums.at[other], sum_send.at[d], sum_recv.at[other], (other, col)
        ).wait_recv()
    for s in range(tiles):
        out = jnp.zeros((width, width), jnp.float32)
        held = jnp.float32(0)
        for t in range(tiles):
            w = (cols[0, s] == col + ncol * t).astype(jnp.float32)
            held = held + w
            total = sums[t // share, t % share]
            for p in range(1, planes):
                total = total + sums[p * CORES + t // share, t % share]
            safe = jnp.where(total > 0, total, 1.0)
            scale = jnp.float32(0.5 * nrow * width) / safe * w
            out = out + result[t] * scale[None, :]
        out_ref[0, s] = out + raw[s].astype(jnp.float32) * (0.5 * held)
    for n in range(CORES * pieces):
        for step in range(planes):

            @pl.when(has_above & (z >= step))
            def _():
                piece(own.at[n], row, 0, up_send.at[step, n], above).wait_send()

            @pl.when(has_below & (z + step < planes))
            def _():
                piece(own.at[n], row, 0, dn_send.at[step, n], below).wait_send()

    for u in range(pieces):
        to_mate(u).wait_send()
    for t in range(tiles):
        for d in along_x + along_y:
            left_out((0, 0), d, t).wait_send()
        for dy, dx in across:
            source, move = ((0, dx), (dy, 0)) if t < half else ((dy, 0), (0, dx))
            left_out(source, move, t).wait_send()
        for c in range(ncol):
            left_copy(c, t, core, mate, left_mate.at[c, t]).wait_send()
    flag_copy.wait_send()
    swap_copy.wait_send()
    for d in range(1, nrow):
        to_row(d).wait_send()


def on_device(nrow, ncol, flow_tiles, tile_cols, pairs):
    _, tiles, _, width = flow_tiles.shape
    planes, depth, share = nrow // CORES, width // SPLIT, tiles // CORES
    pieces = share * SPLIT
    dma = pltpu.SemaphoreType.DMA
    return pl.pallas_call(
        functools.partial(kernel, nrow, ncol),
        out_shape=jax.ShapeDtypeStruct(flow_tiles.shape, jnp.float32),
        in_specs=[pl.BlockSpec(memory_space=pltpu.HBM)] * 2,
        out_specs=pl.BlockSpec(memory_space=pltpu.VMEM),
        scratch_shapes=[
            pltpu.SMEM((1, tiles), jnp.int32),
            pltpu.VMEM((tiles, width, width), jnp.bfloat16),
            pltpu.VMEM((CORES * pieces, depth, width), jnp.bfloat16),
            pltpu.VMEM((nrow, pieces, depth, width), jnp.bfloat16),
            pltpu.VMEM((ncol, tiles, CORES, width, width), jnp.bfloat16),
            pltpu.VMEM((share, CORES, width, width), jnp.float32),
            pltpu.VMEM((share, width, width), jnp.float32),
            pltpu.VMEM((tiles, width, width), jnp.float32),
            pltpu.VMEM((CORES, tiles, width), jnp.float32),
            pltpu.VMEM((nrow, share, width), jnp.float32),
            dma((2,)),
            dma((planes, CORES * pieces)),
            dma((planes, CORES * pieces)),
            dma((pieces,)),
            dma((nrow, pieces)),
            dma((ncol, tiles)),
            dma((CORES, ncol, tiles)),
            dma((ncol, tiles)),
            dma((2,)),
            dma((2,)),
            dma((nrow,)),
            dma((nrow,)),
        ],
        compiler_params=pltpu.CompilerParams(
            collective_id=0, has_side_effects=True, vmem_limit_bytes=24 * 1024 * 1024
        ),
        name="cluster_step",
    )(tile_cols, flow_tiles)


def solution(mesh):
    placed = (P("row", "col", None, None), P("row", "col"), P(("row", "col"), None))
    return jax.shard_map(
        functools.partial(on_device, mesh.shape["row"], mesh.shape["col"]),
        mesh=mesh,
        in_specs=placed,
        out_specs=P("row", "col", None, None),
        check_vma=False,
    )
```

profile of v0, /device:TPU:0, one launch (start us, length us, event | category | flops | bytes accessed | tf_op | source)
XLA Modules:
  0.0 29.8 jit_solution(9763162112491246535)
XLA Ops:
  0.0 0.0 copy-start
  0.0 0.9 %copy-done = bf16[1,2,256,256]{3,2,1,0:T(8,128)(2,1)S(1)} copy-done((bf16[1,2,256,256]{3,2,1,0:T(8,128)(2,1)S(1)}, bf16[1,2,256,256]{3,2,1,0:T(8,128)(2,1)}, u32[]{:S(2)}) %copy-start) | copy-done | bytes 262168
  1.0 0.0 copy-start.1
  1.0 0.7 %copy-done.1 = s32[1,2]{1,0:T(1,128)S(1)} copy-done((s32[1,2]{1,0:T(1,128)S(1)}, s32[1,2]{1,0:T(1,128)}, u32[]{:S(2)}) %copy-start.1) | copy-done | bytes 32
  1.6 27.4 %cluster_step.1 = f32[1,2,256,256]{3,2,1,0:T(8,128)S(1)} custom-call(s32[1,2]{1,0:T(1,128)S(1)} %copy-done.1, bf16[1,2,256,256]{3,2,1,0:T(8,128)(2,1)S(1)} %copy-done), custom_call_target="tpu_custom_call" | custom-call | tf_op jit(solution)/shard_map/cluster_step/pallas_call | solution.py:345
  29.0 0.8 %copy.4 = f32[1,2,256,256]{3,2,1,0:T(8,128)} copy(f32[1,2,256,256]{3,2,1,0:T(8,128)S(1)} %cluster_step.1) | data formatting | bytes 1048576
Async XLA Ops:
  0.0 0.9 %copy-start = (bf16[1,2,256,256]{3,2,1,0:T(8,128)(2,1)S(1)}, bf16[1,2,256,256]{3,2,1,0:T(8,128)(2,1)}, u32[]{:S(2)}) copy-start(bf16[1,2,256,256]{3,2,1,0:T(8,128)(2,1)} %flow_hbm.1) | copy-start | bytes 786436
  1.0 0.7 %copy-start.1 = (s32[1,2]{1,0:T(1,128)S(1)}, s32[1,2]{1,0:T(1,128)}, u32[]{:S(2)}) copy-start(s32[1,2]{1,0:T(1,128)} %cols_hbm.1) | copy-start | bytes 28
where the time goes:
time: 30 us; the launch traced here: 29.8 us
  Pallas kernels  27.4 us (91%)
  local copies, waits for them, and re-layouts  2.4 us (8%)
    pallas_call x1, Pallas kernels, on_device(): pl.pallas_call(functools.partial(kernel, nrow, ncol), out_shape=jax.Shape...  27.4 us
    unnamed x5, local copies, waits for them, and re-layouts  2.4 us

commit v1 on v0

--- a/solution.py
+++ b/solution.py
@@ -375,7 +375,10 @@
             collective_id=0, has_side_effects=True, vmem_limit_bytes=24 * 1024 * 1024
         ),
         name="cluster_step",
-    )(tile_cols, flow_tiles)
+    )(
+        pltpu.with_memory_space_constraint(tile_cols, pltpu.HBM),
+        pltpu.with_memory_space_constraint(flow_tiles, pltpu.HBM),
+    )
 
 
 def solution(mesh):

time: 30 us -> 28.3 us (0.943)
  local copies, waits for them, and re-layouts: 2.4 us -> 0.8 us
    unnamed x5 -> x1, local copies, waits for them, and re-layouts: 2.4 us -> 0.8 us
where the time goes in v1:
time: 28.3 us; the launch traced here: 28.2 us
  Pallas kernels  27.4 us (97%)
  local copies, waits for them, and re-layouts  0.8 us (3%)
    pallas_call x1, Pallas kernels, on_device(): pl.pallas_call(functools.partial(kernel, nrow, ncol), out_shape=jax.Shape...  27.4 us
    unnamed x1, local copies, waits for them, and re-layouts  0.8 us

profile of v1, /device:TPU:0, one launch (start us, length us, event | category | flops | bytes accessed | tf_op | source)
XLA Modules:
  0.0 28.2 jit_solution(6495201553271569958)
XLA Ops:
  0.0 27.4 %cluster_step.1 = f32[1,2,256,256]{3,2,1,0:T(8,128)S(1)} custom-call(s32[1,2]{1,0:T(1,128)} %cols_hbm.1, bf16[1,2,256,256]{3,2,1,0:T(8,128)(2,1)} %flow_hbm.1), custom_call_target="tpu_custom_call" | custom-call | tf_op jit(solution)/shard_map/cluster_step/pallas_call | solution.py:345
  27.4 0.8 %copy.4 = f32[1,2,256,256]{3,2,1,0:T(8,128)} copy(f32[1,2,256,256]{3,2,1,0:T(8,128)S(1)} %cluster_step.1) | data formatting | bytes 1048576

commit v2 on v1

--- a/solution.py
+++ b/solution.py
@@ -27,8 +27,8 @@
 def kernel(
     nrow, ncol, cols_hbm, flow_hbm, out_ref,
     cols, raw, own, blocks, left, acc, swap, result, flags, sums,
-    in_sem, up_send, dn_send, mate_send, recv, left_send, left_recv,
-    left_mate, flag_sem, swap_sem, sum_send, sum_recv,
+    in_sem, z_send, piece_sem, recv, left_send, left_recv, mate_sem,
+    flag_sem, swap_sem, sum_sem,
 ):
     tiles, width = raw.shape[0], raw.shape[2]
     depth = own.shape[1]
@@ -101,25 +101,26 @@
         return remote(src, blocks.at[k, u], send_sem, recv.at[k, u], device)
 
     def arrived(k, u):
-        piece(own.at[u], k, u, mate_send.at[u], mate).wait_recv()
+        piece(own.at[u], k, u, piece_sem, mate).wait_recv()
 
     def to_mate(u):
-        return piece(own.at[(1 - core) * pieces + u], row, u, mate_send.at[u], mate)
-
-    def left_copy(c, t, rc, device, send_sem):
-        part = left.at[c, t, rc]
-        return remote(part, part, send_sem, left_recv.at[rc, c, t], device)
+        return piece(own.at[(1 - core) * pieces + u], row, u, piece_sem, mate)
 
     def left_out(source, move, t):
-        slot = (source[0] + move[0]) * nx + source[1] + move[1]
-        return left_copy(at(*source), t, core, (row, at(*move)), left_send.at[slot, t])
+        c = at(*source)
+        part = left.at[c, t, core]
+        return remote(part, part, left_send, left_recv.at[c, t], (row, at(*move)))
 
     def left_to_mate(source, t):
-        c = at(*source)
-        return left_copy(c, t, core, mate, left_mate.at[c, t])
+        part = left.at[at(*source), t, core]
+        return remote(part, part, mate_sem.at[0], mate_sem.at[1], mate)
+
+    def left_from_mate():
+        part = left.at[:, :, 1 - core]
+        return remote(part, part, mate_sem.at[0], mate_sem.at[1], mate)
 
     def left_arrived(source, t):
-        left_to_mate(source, t).wait_recv()
+        left_out(source, source, t).wait_recv()
         left_to_mate(source, t).start()
 
     def left_relay():
@@ -142,14 +143,14 @@
             @pl.when(has_above)
             def _():
                 piece(
-                    own.at[c * pieces + u], row, u, up_send.at[0, c * pieces + u],
+                    own.at[c * pieces + u], row, u, z_send.at[0],
                     ((z + 1) * CORES + c, col),
                 ).start()
 
             @pl.when(has_below)
             def _():
                 piece(
-                    own.at[c * pieces + u], row, u, dn_send.at[0, c * pieces + u],
+                    own.at[c * pieces + u], row, u, z_send.at[1],
                     ((z - 1) * CORES + c, col),
                 ).start()
 
@@ -180,9 +181,7 @@
 
                     @pl.when(has_above)
                     def _():
-                        piece(
-                            blocks.at[k, u], k, u, up_send.at[step, c * pieces + u], above
-                        ).start()
+                        piece(blocks.at[k, u], k, u, z_send.at[0], above).start()
 
                 @pl.when(z + step < planes)
                 def _():
@@ -191,9 +190,7 @@
 
                     @pl.when(has_below)
                     def _():
-                        piece(
-                            blocks.at[k, u], k, u, dn_send.at[step, c * pieces + u], below
-                        ).start()
+                        piece(blocks.at[k, u], k, u, z_send.at[1], below).start()
 
     def multiply(k):
         a = left[k % ncol, k // ncol].reshape(CORES * width, width)
@@ -242,9 +239,7 @@
             for d in across:
                 for t in range(tiles):
                     left_arrived(d, t)
-            for c in range(ncol):
-                for t in range(tiles):
-                    left_copy(c, t, 1 - core, mate, left_mate.at[c, t]).wait_recv()
+            left_from_mate().wait_recv()
         while done < upto:
             compute(done)
             done += 1
@@ -273,9 +268,13 @@
 
     def to_row(d):
         return remote(
-            sums.at[row], sums.at[row], sum_send.at[d], sum_recv.at[row],
+            sums.at[row], sums.at[row], sum_sem.at[0], sum_sem.at[1],
             ((row + d) % nrow, col),
         )
+
+    def all_sums():
+        part = sums.at[pl.ds(0, nrow - 1)]
+        return remote(part, part, sum_sem.at[0], sum_sem.at[1], mate)
 
     for d in range(1, nrow):
         to_row(d).start()
@@ -292,11 +291,7 @@
         result[core * share + i] = mine * mine
     swap_copy.wait_recv()
 
-    for d in range(1, nrow):
-        other = (row + d) % nrow
-        remote(
-            sums.at[other], sums.at[other], sum_send.at[d], sum_recv.at[other], (other, col)
-        ).wait_recv()
+    all_sums().wait_recv()
     for s in range(tiles):
         out = jnp.zeros((width, width), jnp.float32)
         held = jnp.float32(0)
@@ -310,31 +305,27 @@
             scale = jnp.float32(0.5 * nrow * width) / safe * w
             out = out + result[t] * scale[None, :]
         out_ref[0, s] = out + raw[s].astype(jnp.float32) * (0.5 * held)
-    for n in range(CORES * pieces):
-        for step in range(planes):
-
-            @pl.when(has_above & (z >= step))
-            def _():
-                piece(own.at[n], row, 0, up_send.at[step, n], above).wait_send()
-
-            @pl.when(has_below & (z + step < planes))
-            def _():
-                piece(own.at[n], row, 0, dn_send.at[step, n], below).wait_send()
-
-    for u in range(pieces):
-        to_mate(u).wait_send()
-    for t in range(tiles):
-        for d in along_x + along_y:
-            left_out((0, 0), d, t).wait_send()
-        for dy, dx in across:
-            source, move = ((0, dx), (dy, 0)) if t < half else ((dy, 0), (0, dx))
-            left_out(source, move, t).wait_send()
-        for c in range(ncol):
-            left_copy(c, t, core, mate, left_mate.at[c, t]).wait_send()
+    def sent(number, sem):
+        part = blocks.at[pl.ds(0, number * CORES)]
+        remote(part, part, sem, sem, mate).wait_send()
+
+    for p in range(planes):
+
+        @pl.when(z == p)
+        def _():
+            if p < planes - 1:
+                sent(p + 1, z_send.at[0])
+            if p > 0:
+                sent(planes - p, z_send.at[1])
+
+    part = own.at[pl.ds(0, pieces)]
+    remote(part, part, piece_sem, piece_sem, mate).wait_send()
+    part = left.at[pl.ds(0, ncol - 1), :, core]
+    remote(part, part, left_send, left_send, mate).wait_send()
+    left_from_mate().wait_send()
     flag_copy.wait_send()
     swap_copy.wait_send()
-    for d in range(1, nrow):
-        to_row(d).wait_send()
+    all_sums().wait_send()
 
 
 def on_device(nrow, ncol, flow_tiles, tile_cols, pairs):
@@ -359,17 +350,15 @@
             pltpu.VMEM((CORES, tiles, width), jnp.float32),
             pltpu.VMEM((nrow, share, width), jnp.float32),
             dma((2,)),
-            dma((planes, CORES * pieces)),
-            dma((planes, CORES * pieces)),
-            dma((pieces,)),
+            dma((2,)),
+            dma,
             dma((nrow, pieces)),
+            dma,
             dma((ncol, tiles)),
-            dma((CORES, ncol, tiles)),
-            dma((ncol, tiles)),
-            dma((2,)),
-            dma((2,)),
-            dma((nrow,)),
-            dma((nrow,)),
+            dma((2,)),
+            dma((2,)),
+            dma((2,)),
+            dma((2,)),
         ],
         compiler_params=pltpu.CompilerParams(
             collective_id=0, has_side_effects=True, vmem_limit_bytes=24 * 1024 * 1024

time: 28.3 us -> 27.7 us (0.979)
  Pallas kernels: 27.4 us -> 26.7 us
    pallas_call x1, Pallas kernels: 27.4 us -> 26.7 us  [on_device(): pl.pallas_call(functools.partial(kernel, nrow, ncol), out_shape=jax.Shape...]
where the time goes in v2:
time: 27.7 us; the launch traced here: 27.5 us
  Pallas kernels  26.7 us (96%)
  local copies, waits for them, and re-layouts  0.8 us (3%)
    pallas_call x1, Pallas kernels, on_device(): pl.pallas_call(functools.partial(kernel, nrow, ncol), out_shape=jax.Shape...  26.7 us
    unnamed x1, local copies, waits for them, and re-layouts  0.8 us

profile of v2, /device:TPU:0, one launch (start us, length us, event | category | flops | bytes accessed | tf_op | source)
XLA Modules:
  0.0 27.5 jit_solution(3467578754768039157)
XLA Ops:
  0.0 26.7 %cluster_step.1 = f32[1,2,256,256]{3,2,1,0:T(8,128)S(1)} custom-call(s32[1,2]{1,0:T(1,128)} %cols_hbm.1, bf16[1,2,256,256]{3,2,1,0:T(8,128)(2,1)} %flow_hbm.1), custom_call_target="tpu_custom_call" | custom-call | tf_op jit(solution)/shard_map/cluster_step/pallas_call | solution.py:336
  26.7 0.8 %copy.4 = f32[1,2,256,256]{3,2,1,0:T(8,128)} copy(f32[1,2,256,256]{3,2,1,0:T(8,128)S(1)} %cluster_step.1) | data formatting | bytes 1048576

commit v3 on v2

v3 whole, which is shorter than its diff:
```python
import functools
import math

import jax
import jax.numpy as jnp
from jax import lax
from jax.experimental import pallas as pl
from jax.experimental.pallas import tpu as pltpu
from jax.sharding import PartitionSpec as P

MESH = pl.DeviceIdType.MESH
CORES = 2
SPLIT = 2


def remote(src, dst, send_sem, recv_sem, device):
    return pltpu.make_async_remote_copy(
        src_ref=src,
        dst_ref=dst,
        send_sem=send_sem,
        recv_sem=recv_sem,
        device_id=device,
        device_id_type=MESH,
    )


def kernel(
    nrow, ncol, cols_hbm, flow_hbm, out_ref,
    cols, raw, left, blocks, aid, acc, aid_acc, flags, aid_flags, sums,
    in_sem, z_send, mate_send, recv, mate_recv, left_send, left_recv,
    aid_send, aid_recv, flag_sem, sum_sem,
):
    tiles, width = raw.shape[0], raw.shape[2]
    depth = left.shape[3]
    planes = nrow // CORES
    row, col = lax.axis_index("row"), lax.axis_index("col")
    z, core = row // CORES, row % CORES
    mate_row = row + 1 - 2 * core
    mate = (mate_row, col)
    above, below = (row + CORES, col), (row - CORES, col)
    has_above, has_below = z < planes - 1, z > 0
    ny = math.isqrt(ncol)
    ny = ny if ny * ny == ncol else 1
    nx = ncol // ny
    y, x = col // nx, col % nx
    half = tiles // 2
    top = planes - 1
    is_end = (z == 0) | (z == top)
    is_inside = jnp.logical_not(is_end)
    is_aide = (z == 1) | (z == top - 1)
    end_row = jnp.where(z <= 1, 0, top) * CORES + core
    inner_row = jnp.where(z == 0, 1, top - 1) * CORES + core

    def at(dy, dx):
        return ((y + dy) % ny) * nx + (x + dx) % nx

    along_x = [(0, dx) for dx in range(1, nx)]
    along_y = [(dy, 0) for dy in range(1, ny)]
    beside = along_x + along_y
    across = [(dy, dx) for dy, _ in along_y for _, dx in along_x]
    firsts = [(d, t) for t in range(half) for d in along_x]
    firsts += [(d, t) for t in range(half, tiles) for d in along_y]
    seconds = [(d, t) for t in range(half, tiles) for d in along_x]
    seconds += [(d, t) for t in range(half) for d in along_y]

    load_cols = pltpu.make_async_copy(cols_hbm, cols, in_sem.at[0])
    load_flow = pltpu.make_async_copy(flow_hbm.at[0], raw, in_sem.at[1])
    load_cols.start()
    load_flow.start()

    barrier = pltpu.get_barrier_semaphore()

    def greet(device):
        pl.semaphore_signal(barrier, inc=1, device_id=device, device_id_type=MESH)

    greet(mate)
    for d in beside:
        greet((row, at(*d)))
        greet((mate_row, at(*d)))

    @pl.when(has_above)
    def _():
        for c in range(CORES):
            greet(((z + 1) * CORES + c, col))

    @pl.when(has_below)
    def _():
        for c in range(CORES):
            greet(((z - 1) * CORES + c, col))

    load_cols.wait()
    load_flow.wait()
    for t in range(tiles):
        target = col + ncol * t
        tile = jnp.zeros((width, width), jnp.float32)
        weight = jnp.float32(0)
        for s in range(tiles):
            w = (cols[0, s] == target).astype(jnp.float32)
            weight = weight + w
            tile = tile + raw[s].astype(jnp.float32) * w
        flags[t] = jnp.full((width,), weight, jnp.float32)
        tile = tile.astype(jnp.bfloat16).reshape(SPLIT, depth, width)
        left[col, t] = tile
        blocks[row, t] = tile

    ends = jnp.where(has_above, 1, 0) + jnp.where(has_below, 1, 0)
    pl.semaphore_wait(barrier, 1 + CORES * (len(beside) + ends))

    def piece(src, k, t, h, send_sem, device):
        return remote(src, blocks.at[k, t, h], send_sem, recv.at[k, h], device)

    def arrived(k, h):
        piece(blocks.at[k, core, h], k, core, h, mate_send, mate).wait_recv()

    def late(k, h):
        return mate_recv.at[k if h == 0 else nrow + k % CORES]

    def to_mate(part, arrival):
        return remote(part, part, mate_send, arrival, mate)

    def mate_got(k):
        to_mate(blocks.at[k, 1 - core], mate_recv.at[k]).wait_recv()

    def left_out(source, move, t, h):
        part = left.at[at(*source), t, h]
        arrival = left_recv.at[at(*source), t, h]
        return remote(part, part, left_send, arrival, (row, at(*move)))

    def left_relay(halves):
        for h in halves:
            for d, t in firsts:
                for move in along_y if t < half else along_x:
                    left_out(d, move, t, h).start()

    def left_rest():
        for d, t in seconds:
            for h in range(SPLIT):
                left_out((0, 0), d, t, h).start()

    def aid_up(d, t, h):
        part, arrival = left.at[at(*d), t, h], aid_recv.at[at(*d), t, h]
        return remote(part, aid.at[at(*d), t, h], aid_send, arrival, (inner_row, col))

    def aid_out(halves):
        for h in halves:
            for c in range(CORES):
                part = blocks.at[end_row - core + c, core, h]
                for d in beside:
                    device = (z * CORES + c, at(*d))
                    arrival = aid_recv.at[col, core, h]
                    remote(part, aid.at[col, core, h], aid_send, arrival, device).start()

    def aid_wait(sources, h):
        for d in sources:
            for t in range(tiles):
                part = aid.at[at(*d), t, h]
                remote(part, part, aid_send, aid_recv.at[at(*d), t, h], mate).wait_recv()

    own_to_mate = remote(left.at[col], blocks.at[row], mate_send, mate_recv.at[row], mate)

    def flags_up(device):
        return remote(flags, aid_flags, flag_sem.at[0], flag_sem.at[1], device)

    def own_up(t, h):
        @pl.when(has_above)
        def _():
            device = ((z + 1) * CORES + t, col)
            piece(left.at[col, t, h], row, t, h, z_send.at[0], device).start()

    def own_down(t, h):
        @pl.when(has_below)
        def _():
            device = ((z - 1) * CORES + t, col)
            piece(left.at[col, t, h], row, t, h, z_send.at[1], device).start()

    low = z < top - z
    for h in range(SPLIT):
        for t in range(tiles):

            @pl.when(low)
            def _():
                own_down(t, h)

            own_up(t, h)

            @pl.when(jnp.logical_not(low))
            def _():
                own_down(t, h)

        if h == 0:
            for d, t in firsts:
                for g in range(SPLIT):
                    left_out((0, 0), d, t, g).start()

            @pl.when(is_inside)
            def _():
                left_rest()

    own_to_mate.start()

    @pl.when(is_end)
    def _():
        flags_up((inner_row, col)).start()

    acc[...] = jnp.zeros_like(acc)
    aid_acc[...] = jnp.zeros_like(aid_acc)

    def square(part):
        return part.reshape(-1, width)

    def multiply(*terms):
        for t in range(tiles):
            acc[t] += sum(
                jnp.dot(
                    square(left[c, i]), square(blocks[k, t]), preferred_element_type=jnp.float32
                )
                for k, c, i in terms
            )

    def multiply_piece(k, t, h):
        a = left[k % ncol, k // ncol, :, :, pl.ds(h * depth, depth)]
        acc[t] += jnp.dot(
            a.reshape(width, depth), blocks[k, t, h], preferred_element_type=jnp.float32
        )

    def from_own(k):
        multiply((k, k % ncol, k // ncol))

    def is_direct(k):
        c = k % ncol
        return (c // nx == y) | (c % nx == x)

    def planes_at(distance, body):
        for sign in (-1, 1) if distance else (1,):
            plane = z + sign * distance
            pl.when((plane >= 0) & (plane < planes))(functools.partial(body, plane))

    def direct_products(distance):
        def run(plane):
            for c in range(CORES):
                k = plane * CORES + c
                if distance:
                    mate_got(k)

                @pl.when(is_direct(k))
                def _():
                    from_own(k)

        planes_at(distance, run)

    def mate_own_got():
        remote(left.at[col], blocks.at[mate_row], mate_send, mate_recv.at[mate_row], mate).wait_recv()

    fillers = []

    def first_filler():
        mate_own_got()
        direct_products(0)

    if planes > 3:
        fillers.append(first_filler)
        for distance in range(1, planes - 2):
            fillers.append(functools.partial(direct_products, distance))

    def relay(step):
        for h in range(SPLIT):
            if step == 1 and h == SPLIT - 1:
                for g in range(SPLIT):
                    for d, t in firsts:
                        left_out(d, d, t, g).wait_recv()
                    if g < SPLIT // 2:
                        left_relay([g])
                    else:
                        pl.when(jnp.logical_not(is_aide))(functools.partial(left_relay, [g]))
                pl.when(is_end)(left_rest)

            for c in range(CORES):
                if step == planes - 2:
                    number = SPLIT * CORES - (h * CORES + c)
                    for _ in range(-(-len(fillers) // number)):
                        pl.when(is_inside)(fillers.pop(0))
                for sign in (-1, 1):
                    plane = z + sign * step

                    @pl.when(is_inside & (plane >= 0) & (plane < planes))
                    def _():
                        k = plane * CORES + c
                        part = blocks.at[k, core, h]
                        arrived(k, h)
                        if sign < 0:
                            piece(part, k, core, h, z_send.at[0], above).start()
                        else:
                            piece(part, k, core, h, z_send.at[1], below).start()
                        to_mate(part, mate_recv.at[k]).start()

    for step in range(1, planes - 1):
        relay(step)
        if step == 1:

            @pl.when(is_aide)
            def _():
                aid_out(range(SPLIT // 2))
                left_relay(range(SPLIT // 2, SPLIT))
                aid_out(range(SPLIT // 2, SPLIT))

            @pl.when(is_end)
            def _():
                for h in range(SPLIT):
                    for t in range(tiles):
                        for d in across:
                            left_out(d, d, t, h).wait_recv()
                            aid_up(d, t, h).start()

            for d, t in seconds:
                for h in range(SPLIT):
                    left_out(d, d, t, h).wait_recv()

    def to_row(slot, d):
        part = sums.at[slot]
        return remote(part, part, sum_sem.at[0], sum_sem.at[1], ((row + d) % nrow, col))

    def some_sums(number):
        part = sums.at[pl.ds(0, number)]
        return remote(part, part, sum_sem.at[0], sum_sem.at[1], mate)

    def send_sums(slot, values, weights):
        for t in range(tiles):
            sums[slot, t] = jnp.sum(values[t] * values[t], axis=0) * weights[t]
        for d in range(1, nrow):
            to_row(slot, d).start()

    def aid_own():
        for t in range(tiles):
            k = col + ncol * t
            for i in range(tiles):
                aid_acc[i] += jnp.dot(
                    square(blocks[end_row, t]), square(blocks[k, i]),
                    preferred_element_type=jnp.float32,
                )

    def aid_multiply(sources, h):
        aid_wait(sources, h)
        if sources:
            for i in range(tiles):
                aid_acc[i, pl.ds(h * depth, depth)] += sum(
                    jnp.dot(
                        aid[at(*d), t, h], square(blocks[at(*d) + ncol * t, i]),
                        preferred_element_type=jnp.float32,
                    )
                    for d in sources
                    for t in range(tiles)
                )

    def inside():
        direct_products(planes - 2)

        @pl.when(is_aide)
        def _():
            aid_own()
            for h in range(SPLIT // 2):
                aid_multiply(beside + across, h)
            for h in range(SPLIT // 2, SPLIT):
                aid_multiply(across, h)

        for d in across:
            for t in range(tiles):
                for h in range(SPLIT):
                    left_out(d, d, t, h).wait_recv()
        if across:
            multiply(*((at(*d) + ncol * t, at(*d), t) for d in across for t in range(tiles)))
        send_sums(row, acc, flags)

        @pl.when(is_aide)
        def _():
            for h in range(SPLIT // 2, SPLIT):
                aid_multiply(beside, h)
            flags_up(mate).wait_recv()
            send_sums(end_row, aid_acc, aid_flags)

    def outside():
        mate_own_got()

        def near(plane):
            for c in range(CORES):
                from_own(plane * CORES + c)

        planes_at(0, near)

        def nearer(plane):
            for h in range(SPLIT):
                for c in range(CORES):
                    k = plane * CORES + c
                    arrived(k, h)
                    to_mate(blocks.at[k, core, h], mate_recv.at[k]).start()
            for c in range(CORES):
                mate_got(plane * CORES + c)
                from_own(plane * CORES + c)

        for distance in range(1, top):
            planes_at(distance, nearer)

        def farthest(plane):
            for h in range(SPLIT):
                for c in range(CORES):
                    k = plane * CORES + c
                    arrived(k, h)
                    to_mate(blocks.at[k, core, h], late(k, h)).start()
                    multiply_piece(k, core, h)
            for h in range(SPLIT):
                for c in range(CORES):
                    k = plane * CORES + c
                    to_mate(blocks.at[k, 1 - core, h], late(k, h)).wait_recv()
                    multiply_piece(k, 1 - core, h)

        planes_at(top, farthest)

    pl.when(is_inside)(inside)
    pl.when(is_end)(outside)

    @pl.when(is_end)
    def _():
        some_sums(nrow).wait_recv()

    @pl.when(is_aide)
    def _():
        some_sums(nrow - 2).wait_recv()

    if planes > 4:

        @pl.when(jnp.logical_not(is_end | is_aide))
        def _():
            some_sums(nrow - 1).wait_recv()

    for s in range(tiles):
        out = jnp.zeros((width, width), jnp.float32)
        held = jnp.float32(0)
        for t in range(tiles):
            w = (cols[0, s] == col + ncol * t).astype(jnp.float32)
            held = held + w
            total = sums[0, t]
            for k in range(1, nrow):
                total = total + sums[k, t]
            safe = jnp.where(total > 0, total, 1.0)
            scale = jnp.float32(0.5 * nrow * width) / safe * w
            out = out + acc[t] * acc[t] * scale[None, :]
        out_ref[0, s] = out + raw[s].astype(jnp.float32) * (0.5 * held)

    def sent(part, sem):
        remote(part, part, sem, sem, mate).wait_send()

    for p in range(planes):

        @pl.when(z == p)
        def _():
            if p < top:
                sent(blocks.at[pl.ds(0, (p + 1) * CORES), 0], z_send.at[0])
            if p > 0:
                sent(blocks.at[pl.ds(0, (planes - p) * CORES), 0], z_send.at[1])

    sent(blocks.at[:, 0], mate_send)
    sent(left.at[pl.ds(0, ncol - 1)], left_send)

    @pl.when(is_end)
    def _():
        if across:
            sent(aid.at[pl.ds(0, len(across))], aid_send)
        flags_up(mate).wait_send()

    @pl.when(is_inside)
    def _():
        some_sums(nrow - 1).wait_send()

    @pl.when(is_aide)
    def _():
        some_sums(nrow - 1).wait_send()
        sent(aid.at[pl.ds(0, len(beside))], aid_send)


def on_device(nrow, ncol, flow_tiles, tile_cols, pairs):
    _, tiles, _, width = flow_tiles.shape
    depth = width // SPLIT
    dma = pltpu.SemaphoreType.DMA
    return pl.pallas_call(
        functools.partial(kernel, nrow, ncol),
        out_shape=jax.ShapeDtypeStruct(flow_tiles.shape, jnp.float32),
        in_specs=[pl.BlockSpec(memory_space=pltpu.HBM)] * 2,
        out_specs=pl.BlockSpec(memory_space=pltpu.VMEM),
        scratch_shapes=[
            pltpu.SMEM((1, tiles), jnp.int32),
            pltpu.VMEM((tiles, width, width), jnp.bfloat16),
            pltpu.VMEM((ncol, tiles, SPLIT, depth, width), jnp.bfloat16),
            pltpu.VMEM((nrow, tiles, SPLIT, depth, width), jnp.bfloat16),
            pltpu.VMEM((ncol, tiles, SPLIT, depth, width), jnp.bfloat16),
            pltpu.VMEM((tiles, width, width), jnp.float32),
            pltpu.VMEM((tiles, width, width), jnp.float32),
            pltpu.VMEM((tiles, width), jnp.float32),
            pltpu.VMEM((tiles, width), jnp.float32),
            pltpu.VMEM((nrow, tiles, width), jnp.float32),
            dma((2,)),
            dma((2,)),
            dma,
            dma((nrow, SPLIT)),
            dma((nrow + CORES,)),
            dma,
            dma((ncol, tiles, SPLIT)),
            dma,
            dma((ncol, tiles, SPLIT)),
            dma((2,)),
            dma((2,)),
        ],
        compiler_params=pltpu.CompilerParams(
            collective_id=0, has_side_effects=True, vmem_limit_bytes=24 * 1024 * 1024
        ),
        name="cluster_step",
    )(
        pltpu.with_memory_space_constraint(tile_cols, pltpu.HBM),
        pltpu.with_memory_space_constraint(flow_tiles, pltpu.HBM),
    )


def solution(mesh):
    placed = (P("row", "col", None, None), P("row", "col"), P(("row", "col"), None))
    return jax.shard_map(
        functools.partial(on_device, mesh.shape["row"], mesh.shape["col"]),
        mesh=mesh,
        in_specs=placed,
        out_specs=P("row", "col", None, None),
        check_vma=False,
    )
```

time: 27.7 us -> 26 us (0.939)
  Pallas kernels: 26.7 us -> 25 us
    pallas_call x1, Pallas kernels: 26.7 us -> 25 us  [on_device(): pl.pallas_call(functools.partial(kernel, nrow, ncol), out_shape=jax.Shape...]
where the time goes in v3:
time: 26 us; the launch traced here: 25.8 us
  Pallas kernels  25 us (96%)
  local copies, waits for them, and re-layouts  0.8 us (3%)
    pallas_call x1, Pallas kernels, on_device(): pl.pallas_call(functools.partial(kernel, nrow, ncol), out_shape=jax.Shape...  25 us
    unnamed x1, local copies, waits for them, and re-layouts  0.8 us

profile of v3, /device:TPU:0, one launch (start us, length us, event | category | flops | bytes accessed | tf_op | source)
XLA Modules:
  0.0 25.8 jit_solution(17951092774775043823)
XLA Ops:
  0.0 25.0 %cluster_step.1 = f32[1,2,256,256]{3,2,1,0:T(8,128)S(1)} custom-call(s32[1,2]{1,0:T(1,128)} %cols_hbm.1, bf16[1,2,256,256]{3,2,1,0:T(8,128)(2,1)} %flow_hbm.1), custom_call_target="tpu_custom_call" | custom-call | tf_op jit(solution)/shard_map/cluster_step/pallas_call | solution.py:483
  25.0 0.8 %copy.4 = f32[1,2,256,256]{3,2,1,0:T(8,128)} copy(f32[1,2,256,256]{3,2,1,0:T(8,128)S(1)} %cluster_step.1) | data formatting | bytes 1048576

commit v4 on v3

--- a/solution.py
+++ b/solution.py
@@ -62,6 +62,8 @@
     firsts += [(d, t) for t in range(half, tiles) for d in along_y]
     seconds = [(d, t) for t in range(half, tiles) for d in along_x]
     seconds += [(d, t) for t in range(half) for d in along_y]
+    topped = nx == ny and tiles == CORES
+    kept = depth // 4
 
     load_cols = pltpu.make_async_copy(cols_hbm, cols, in_sem.at[0])
     load_flow = pltpu.make_async_copy(flow_hbm.at[0], raw, in_sem.at[1])
@@ -106,25 +108,43 @@
     ends = jnp.where(has_above, 1, 0) + jnp.where(has_below, 1, 0)
     pl.semaphore_wait(barrier, 1 + CORES * (len(beside) + ends))
 
-    def piece(src, k, t, h, send_sem, device):
-        return remote(src, blocks.at[k, t, h], send_sem, recv.at[k, h], device)
-
-    def arrived(k, h):
-        piece(blocks.at[k, core, h], k, core, h, mate_send, mate).wait_recv()
-
-    def late(k, h):
-        return mate_recv.at[k if h == 0 else nrow + k % CORES]
+    def piece(src, k, t, h, up, device):
+        index = k if up else k - CORES
+        send_sem = z_send.at[0 if up else 1]
+        return remote(src, blocks.at[k, t, h], send_sem, recv.at[index, h], device)
+
+    def arrived(k, h, up):
+        piece(blocks.at[k, core, h], k, core, h, up, mate).wait_recv()
 
     def to_mate(part, arrival):
         return remote(part, part, mate_send, arrival, mate)
 
-    def mate_got(k):
-        to_mate(blocks.at[k, 1 - core], mate_recv.at[k]).wait_recv()
+    def mate_got(plane):
+        part = blocks.at[pl.ds(plane * CORES, CORES), 1 - core]
+        to_mate(part, mate_recv.at[plane]).wait_recv()
+
+    def late(plane, h):
+        return mate_recv.at[plane if h == 0 else top + h]
+
+    def got(part, sem):
+        remote(part, part, sem, sem, mate).wait_recv()
 
     def left_out(source, move, t, h):
         part = left.at[at(*source), t, h]
-        arrival = left_recv.at[at(*source), t, h]
-        return remote(part, part, left_send, arrival, (row, at(*move)))
+        if source != (0, 0):
+            kind = SPLIT + h
+        else:
+            kind = h if (move, t) in firsts else 2 * SPLIT
+        return remote(part, part, left_send, left_recv.at[kind], (row, at(*move)))
+
+    def first_got(h):
+        got(left.at[pl.ds(0, len(firsts)), 0, 0], left_recv.at[h])
+
+    def second_got():
+        got(left.at[pl.ds(0, len(seconds)), 0], left_recv.at[2 * SPLIT])
+
+    def across_got(h):
+        got(left.at[pl.ds(0, len(across)), :, 0], left_recv.at[SPLIT + h])
 
     def left_relay(halves):
         for h in halves:
@@ -138,25 +158,53 @@
                 left_out((0, 0), d, t, h).start()
 
     def aid_up(d, t, h):
-        part, arrival = left.at[at(*d), t, h], aid_recv.at[at(*d), t, h]
-        return remote(part, aid.at[at(*d), t, h], aid_send, arrival, (inner_row, col))
+        part = left.at[at(*d), t, h]
+        arrival = aid_recv.at[SPLIT + h]
+        return remote(part, aid.at[at(*d), t, h], aid_send.at[0], arrival, (inner_row, col))
+
+    def top_up():
+        for d, t in firsts:
+            part = left.at[at(*d), t, SPLIT - 1, pl.ds(kept, depth - kept)]
+            target = aid.at[at(*d), t, SPLIT - 1, pl.ds(kept, depth - kept)]
+            arrival = aid_recv.at[2 * SPLIT]
+            remote(part, target, aid_send.at[1], arrival, (inner_row, col)).start()
 
     def aid_out(halves):
+        def send(h, c, sources, number=depth, sem=aid_send.at[0], arrival=None):
+            part = blocks.at[end_row - core + c, core, h, pl.ds(0, number)]
+            target = aid.at[col, core, h, pl.ds(0, number)]
+            for d in sources:
+                device = (z * CORES + c, at(*d))
+                remote(part, target, sem, arrival or aid_recv.at[h], device).start()
+
+        def send_late(h, c, by_top, others):
+            send(h, c, others)
+            send(h, c, by_top, kept, aid_send.at[2], aid_recv.at[2 * SPLIT + 1])
+
         for h in halves:
             for c in range(CORES):
-                part = blocks.at[end_row - core + c, core, h]
-                for d in beside:
-                    device = (z * CORES + c, at(*d))
-                    arrival = aid_recv.at[col, core, h]
-                    remote(part, aid.at[col, core, h], aid_send, arrival, device).start()
-
-    def aid_wait(sources, h):
-        for d in sources:
-            for t in range(tiles):
-                part = aid.at[at(*d), t, h]
-                remote(part, part, aid_send, aid_recv.at[at(*d), t, h], mate).wait_recv()
-
-    own_to_mate = remote(left.at[col], blocks.at[row], mate_send, mate_recv.at[row], mate)
+                if topped and h == SPLIT - 1:
+                    pl.when(core < half)(functools.partial(send_late, h, c, along_x, along_y))
+                    pl.when(core >= half)(functools.partial(send_late, h, c, along_y, along_x))
+                else:
+                    send(h, c, beside)
+
+    by_top = aid.at[pl.ds(0, len(beside)), 0, 0, pl.ds(kept, depth - kept)]
+    not_by_top = aid.at[pl.ds(0, len(beside)), 0, 0, pl.ds(0, kept)]
+
+    def aid_beside_got(h):
+        if topped and h == SPLIT - 1:
+            got(by_top, aid_recv.at[2 * SPLIT])
+            got(aid.at[pl.ds(0, len(beside)), 0, 0], aid_recv.at[h])
+            got(not_by_top, aid_recv.at[2 * SPLIT + 1])
+        else:
+            got(aid.at[pl.ds(0, len(beside)), :, 0], aid_recv.at[h])
+
+    def aid_across_got(h):
+        if across:
+            got(aid.at[pl.ds(0, len(across)), :, 0], aid_recv.at[SPLIT + h])
+
+    own_to_mate = remote(left.at[col], blocks.at[row], mate_send, mate_recv.at[z], mate)
 
     def flags_up(device):
         return remote(flags, aid_flags, flag_sem.at[0], flag_sem.at[1], device)
@@ -165,13 +213,13 @@
         @pl.when(has_above)
         def _():
             device = ((z + 1) * CORES + t, col)
-            piece(left.at[col, t, h], row, t, h, z_send.at[0], device).start()
+            piece(left.at[col, t, h], row, t, h, True, device).start()
 
     def own_down(t, h):
         @pl.when(has_below)
         def _():
             device = ((z - 1) * CORES + t, col)
-            piece(left.at[col, t, h], row, t, h, z_send.at[1], device).start()
+            piece(left.at[col, t, h], row, t, h, False, device).start()
 
     low = z < top - z
     for h in range(SPLIT):
@@ -237,10 +285,10 @@
 
     def direct_products(distance):
         def run(plane):
+            if distance:
+                mate_got(plane)
             for c in range(CORES):
                 k = plane * CORES + c
-                if distance:
-                    mate_got(k)
 
                 @pl.when(is_direct(k))
                 def _():
@@ -249,7 +297,7 @@
         planes_at(distance, run)
 
     def mate_own_got():
-        remote(left.at[col], blocks.at[mate_row], mate_send, mate_recv.at[mate_row], mate).wait_recv()
+        got(blocks.at[mate_row], mate_recv.at[z])
 
     fillers = []
 
@@ -266,12 +314,13 @@
         for h in range(SPLIT):
             if step == 1 and h == SPLIT - 1:
                 for g in range(SPLIT):
-                    for d, t in firsts:
-                        left_out(d, d, t, g).wait_recv()
+                    first_got(g)
                     if g < SPLIT // 2:
                         left_relay([g])
                     else:
                         pl.when(jnp.logical_not(is_aide))(functools.partial(left_relay, [g]))
+                if topped:
+                    pl.when(is_end)(top_up)
                 pl.when(is_end)(left_rest)
 
             for c in range(CORES):
@@ -286,12 +335,9 @@
                     def _():
                         k = plane * CORES + c
                         part = blocks.at[k, core, h]
-                        arrived(k, h)
-                        if sign < 0:
-                            piece(part, k, core, h, z_send.at[0], above).start()
-                        else:
-                            piece(part, k, core, h, z_send.at[1], below).start()
-                        to_mate(part, mate_recv.at[k]).start()
+                        arrived(k, h, sign < 0)
+                        piece(part, k, core, h, sign < 0, above if sign < 0 else below).start()
+                        to_mate(part, mate_recv.at[plane]).start()
 
     for step in range(1, planes - 1):
         relay(step)
@@ -306,18 +352,18 @@
             @pl.when(is_end)
             def _():
                 for h in range(SPLIT):
+                    if across:
+                        across_got(h)
                     for t in range(tiles):
                         for d in across:
-                            left_out(d, d, t, h).wait_recv()
                             aid_up(d, t, h).start()
 
-            for d, t in seconds:
-                for h in range(SPLIT):
-                    left_out(d, d, t, h).wait_recv()
+            second_got()
 
     def to_row(slot, d):
         part = sums.at[slot]
-        return remote(part, part, sum_sem.at[0], sum_sem.at[1], ((row + d) % nrow, col))
+        device = ((row + jnp.where(low, d, nrow - d)) % nrow, col)
+        return remote(part, part, sum_sem.at[0], sum_sem.at[1], device)
 
     def some_sums(number):
         part = sums.at[pl.ds(0, number)]
@@ -339,7 +385,6 @@
                 )
 
     def aid_multiply(sources, h):
-        aid_wait(sources, h)
         if sources:
             for i in range(tiles):
                 aid_acc[i, pl.ds(h * depth, depth)] += sum(
@@ -358,22 +403,25 @@
         def _():
             aid_own()
             for h in range(SPLIT // 2):
-                aid_multiply(beside + across, h)
-            for h in range(SPLIT // 2, SPLIT):
+                aid_beside_got(h)
+                aid_multiply(beside, h)
+            for h in range(SPLIT // 2):
+                aid_across_got(h)
                 aid_multiply(across, h)
 
-        for d in across:
-            for t in range(tiles):
-                for h in range(SPLIT):
-                    left_out(d, d, t, h).wait_recv()
         if across:
+            for h in range(SPLIT):
+                across_got(h)
             multiply(*((at(*d) + ncol * t, at(*d), t) for d in across for t in range(tiles)))
         send_sums(row, acc, flags)
 
         @pl.when(is_aide)
         def _():
             for h in range(SPLIT // 2, SPLIT):
+                aid_beside_got(h)
                 aid_multiply(beside, h)
+                aid_across_got(h)
+                aid_multiply(across, h)
             flags_up(mate).wait_recv()
             send_sums(end_row, aid_acc, aid_flags)
 
@@ -386,33 +434,32 @@
 
         planes_at(0, near)
 
-        def nearer(plane):
+        def nearer(up, plane):
             for h in range(SPLIT):
                 for c in range(CORES):
                     k = plane * CORES + c
-                    arrived(k, h)
-                    to_mate(blocks.at[k, core, h], mate_recv.at[k]).start()
+                    arrived(k, h, up)
+                    to_mate(blocks.at[k, core, h], mate_recv.at[plane]).start()
+            mate_got(plane)
             for c in range(CORES):
-                mate_got(plane * CORES + c)
                 from_own(plane * CORES + c)
 
-        for distance in range(1, top):
-            planes_at(distance, nearer)
-
-        def farthest(plane):
+        def farthest(up, plane):
             for h in range(SPLIT):
                 for c in range(CORES):
                     k = plane * CORES + c
-                    arrived(k, h)
-                    to_mate(blocks.at[k, core, h], late(k, h)).start()
+                    arrived(k, h, up)
+                    to_mate(blocks.at[k, core, h], late(plane, h)).start()
                     multiply_piece(k, core, h)
             for h in range(SPLIT):
+                got(blocks.at[pl.ds(plane * CORES, CORES), 1 - core, h], late(plane, h))
                 for c in range(CORES):
-                    k = plane * CORES + c
-                    to_mate(blocks.at[k, 1 - core, h], late(k, h)).wait_recv()
-                    multiply_piece(k, 1 - core, h)
-
-        planes_at(top, farthest)
+                    multiply_piece(plane * CORES + c, 1 - core, h)
+
+        for distance in range(1, planes):
+            body = nearer if distance < top else farthest
+            pl.when(z == 0)(functools.partial(body, False, distance))
+            pl.when(z == top)(functools.partial(body, True, top - distance))
 
     pl.when(is_inside)(inside)
     pl.when(is_end)(outside)
@@ -432,18 +479,21 @@
             some_sums(nrow - 1).wait_recv()
 
     for s in range(tiles):
-        out = jnp.zeros((width, width), jnp.float32)
-        held = jnp.float32(0)
+        held, slot = jnp.float32(0), jnp.int32(0)
         for t in range(tiles):
-            w = (cols[0, s] == col + ncol * t).astype(jnp.float32)
-            held = held + w
-            total = sums[0, t]
+            match = cols[0, s] == col + ncol * t
+            held = held + match.astype(jnp.float32)
+            slot = slot + match.astype(jnp.int32) * t
+        total = jnp.zeros((width,), jnp.float32)
+        for t in range(tiles):
+            part = sums[0, t]
             for k in range(1, nrow):
-                total = total + sums[k, t]
-            safe = jnp.where(total > 0, total, 1.0)
-            scale = jnp.float32(0.5 * nrow * width) / safe * w
-            out = out + acc[t] * acc[t] * scale[None, :]
-        out_ref[0, s] = out + raw[s].astype(jnp.float32) * (0.5 * held)
+                part = part + sums[k, t]
+            total = total + part * (slot == t).astype(jnp.float32)
+        safe = jnp.where(total > 0, total, 1.0)
+        scale = jnp.float32(0.5 * nrow * width) / safe * held
+        value = acc[slot]
+        out_ref[0, s] = value * value * scale[None, :] + raw[s].astype(jnp.float32) * (0.5 * held)
 
     def sent(part, sem):
         remote(part, part, sem, sem, mate).wait_send()
@@ -463,7 +513,9 @@
     @pl.when(is_end)
     def _():
         if across:
-            sent(aid.at[pl.ds(0, len(across))], aid_send)
+            sent(blocks.at[pl.ds(0, len(across) * tiles), 0], aid_send.at[0])
+        if topped:
+            sent(by_top, aid_send.at[1])
         flags_up(mate).wait_send()
 
     @pl.when(is_inside)
@@ -473,7 +525,11 @@
     @pl.when(is_aide)
     def _():
         some_sums(nrow - 1).wait_send()
-        sent(aid.at[pl.ds(0, len(beside))], aid_send)
+        if topped:
+            sent(blocks.at[pl.ds(0, 3 * len(along_x)), 0], aid_send.at[0])
+            sent(not_by_top, aid_send.at[2])
+        else:
+            sent(blocks.at[pl.ds(0, len(beside) * CORES), 0], aid_send.at[0])
 
 
 def on_device(nrow, ncol, flow_tiles, tile_cols, pairs):
@@ -499,12 +555,12 @@
             dma((2,)),
             dma((2,)),
             dma,
-            dma((nrow, SPLIT)),
-            dma((nrow + CORES,)),
+            dma((nrow - CORES, SPLIT)),
+            dma((nrow // CORES + SPLIT - 1,)),
             dma,
-            dma((ncol, tiles, SPLIT)),
-            dma,
-            dma((ncol, tiles, SPLIT)),
+            dma((2 * SPLIT + 1,)),
+            dma((3,)),
+            dma((2 * SPLIT + 2,)),
             dma((2,)),
             dma((2,)),
         ],

time: 26 us -> 24.9 us (0.958)
  Pallas kernels: 25 us -> 24 us
    pallas_call x1, Pallas kernels: 25 us -> 24 us  [on_device(): pl.pallas_call(functools.partial(kernel, nrow, ncol), out_shape=jax.Shape...]
where the time goes in v4:
time: 24.9 us; the launch traced here: 24.8 us
  Pallas kernels  24 us (96%)
  local copies, waits for them, and re-layouts  0.8 us (3%)
    pallas_call x1, Pallas kernels, on_device(): pl.pallas_call(functools.partial(kernel, nrow, ncol), out_shape=jax.Shape...  24 us
    unnamed x1, local copies, waits for them, and re-layouts  0.8 us

profile of v4, /device:TPU:0, one launch (start us, length us, event | category | flops | bytes accessed | tf_op | source)
XLA Modules:
  0.0 24.8 jit_solution(8917043070372636949)
XLA Ops:
  0.0 24.0 %cluster_step.1 = f32[1,2,256,256]{3,2,1,0:T(8,128)S(1)} custom-call(s32[1,2]{1,0:T(1,128)} %cols_hbm.1, bf16[1,2,256,256]{3,2,1,0:T(8,128)(2,1)} %flow_hbm.1), custom_call_target="tpu_custom_call" | custom-call | tf_op jit(solution)/shard_map/cluster_step/pallas_call | solution.py:539
  24.0 0.8 %copy.4 = f32[1,2,256,256]{3,2,1,0:T(8,128)} copy(f32[1,2,256,256]{3,2,1,0:T(8,128)S(1)} %cluster_step.1) | data formatting | bytes 1048576

commit v5 on v4

--- a/solution.py
+++ b/solution.py
@@ -27,8 +27,8 @@
 def kernel(
     nrow, ncol, cols_hbm, flow_hbm, out_ref,
     cols, raw, left, blocks, aid, acc, aid_acc, flags, aid_flags, sums,
-    in_sem, z_send, mate_send, recv, mate_recv, left_send, left_recv,
-    aid_send, aid_recv, flag_sem, sum_sem,
+    z_send, mate_send, recv, mate_recv, left_send, left_recv,
+    aid_send, aid_recv, sum_sem, last_sem,
 ):
     tiles, width = raw.shape[0], raw.shape[2]
     depth = left.shape[3]
@@ -64,9 +64,10 @@
     seconds += [(d, t) for t in range(half) for d in along_y]
     topped = nx == ny and tiles == CORES
     kept = depth // 4
-
-    load_cols = pltpu.make_async_copy(cols_hbm, cols, in_sem.at[0])
-    load_flow = pltpu.make_async_copy(flow_hbm.at[0], raw, in_sem.at[1])
+    spare = kept
+
+    load_cols = pltpu.make_async_copy(cols_hbm, cols, left_send)
+    load_flow = pltpu.make_async_copy(flow_hbm.at[0], raw, mate_send)
     load_cols.start()
     load_flow.start()
 
@@ -110,21 +111,36 @@
 
     def piece(src, k, t, h, up, device):
         index = k if up else k - CORES
-        send_sem = z_send.at[0 if up else 1]
+        send_sem = z_send
         return remote(src, blocks.at[k, t, h], send_sem, recv.at[index, h], device)
 
     def arrived(k, h, up):
         piece(blocks.at[k, core, h], k, core, h, up, mate).wait_recv()
 
-    def to_mate(part, arrival):
-        return remote(part, part, mate_send, arrival, mate)
+    def last_piece(k, up, device):
+        send_sem = z_send
+        body, rest = last_body(k, core), last_rest(k, core)
+        index = k if up else k - CORES
+        remote(body, body, send_sem, recv.at[index, SPLIT - 1], device).start()
+        remote(rest, rest, send_sem, last_sem.at[0], device).start()
+        other = (device[0] + 1 - 2 * core, col)
+        remote(rest, rest, aid_send.at[1], last_sem.at[1], other).start()
+
+    def last_body(k, t):
+        return blocks.at[k, t, SPLIT - 1, pl.ds(0, depth - spare)]
+
+    def last_rest(k, t):
+        return blocks.at[k, t, SPLIT - 1, pl.ds(depth - spare, spare)]
+
+    def to_mate(part, arrival, sem=mate_send):
+        return remote(part, part, sem, arrival, mate)
 
     def mate_got(plane):
         part = blocks.at[pl.ds(plane * CORES, CORES), 1 - core]
         to_mate(part, mate_recv.at[plane]).wait_recv()
 
-    def late(plane, h):
-        return mate_recv.at[plane if h == 0 else top + h]
+    def late(plane, h, c):
+        return mate_recv.at[plane if h == 0 else top + (h - 1) * CORES + c + 1]
 
     def got(part, sem):
         remote(part, part, sem, sem, mate).wait_recv()
@@ -166,20 +182,20 @@
         for d, t in firsts:
             part = left.at[at(*d), t, SPLIT - 1, pl.ds(kept, depth - kept)]
             target = aid.at[at(*d), t, SPLIT - 1, pl.ds(kept, depth - kept)]
-            arrival = aid_recv.at[2 * SPLIT]
+            arrival = aid_recv.at[SPLIT - 1]
             remote(part, target, aid_send.at[1], arrival, (inner_row, col)).start()
 
     def aid_out(halves):
-        def send(h, c, sources, number=depth, sem=aid_send.at[0], arrival=None):
+        def send(h, c, sources, number=depth, sem=aid_send.at[0]):
             part = blocks.at[end_row - core + c, core, h, pl.ds(0, number)]
             target = aid.at[col, core, h, pl.ds(0, number)]
             for d in sources:
                 device = (z * CORES + c, at(*d))
-                remote(part, target, sem, arrival or aid_recv.at[h], device).start()
+                remote(part, target, sem, aid_recv.at[h], device).start()
 
         def send_late(h, c, by_top, others):
             send(h, c, others)
-            send(h, c, by_top, kept, aid_send.at[2], aid_recv.at[2 * SPLIT + 1])
+            send(h, c, by_top, kept, aid_send.at[1])
 
         for h in halves:
             for c in range(CORES):
@@ -189,25 +205,14 @@
                 else:
                     send(h, c, beside)
 
-    by_top = aid.at[pl.ds(0, len(beside)), 0, 0, pl.ds(kept, depth - kept)]
-    not_by_top = aid.at[pl.ds(0, len(beside)), 0, 0, pl.ds(0, kept)]
-
     def aid_beside_got(h):
-        if topped and h == SPLIT - 1:
-            got(by_top, aid_recv.at[2 * SPLIT])
-            got(aid.at[pl.ds(0, len(beside)), 0, 0], aid_recv.at[h])
-            got(not_by_top, aid_recv.at[2 * SPLIT + 1])
-        else:
-            got(aid.at[pl.ds(0, len(beside)), :, 0], aid_recv.at[h])
+        got(aid.at[pl.ds(0, len(beside)), :, 0], aid_recv.at[h])
 
     def aid_across_got(h):
         if across:
             got(aid.at[pl.ds(0, len(across)), :, 0], aid_recv.at[SPLIT + h])
 
     own_to_mate = remote(left.at[col], blocks.at[row], mate_send, mate_recv.at[z], mate)
-
-    def flags_up(device):
-        return remote(flags, aid_flags, flag_sem.at[0], flag_sem.at[1], device)
 
     def own_up(t, h):
         @pl.when(has_above)
@@ -245,10 +250,6 @@
                 left_rest()
 
     own_to_mate.start()
-
-    @pl.when(is_end)
-    def _():
-        flags_up((inner_row, col)).start()
 
     acc[...] = jnp.zeros_like(acc)
     aid_acc[...] = jnp.zeros_like(aid_acc)
@@ -336,7 +337,11 @@
                         k = plane * CORES + c
                         part = blocks.at[k, core, h]
                         arrived(k, h, sign < 0)
-                        piece(part, k, core, h, sign < 0, above if sign < 0 else below).start()
+                        device = above if sign < 0 else below
+                        if (step, c, h) == (planes - 2, CORES - 1, SPLIT - 1):
+                            last_piece(k, sign < 0, device)
+                        else:
+                            piece(part, k, core, h, sign < 0, device).start()
                         to_mate(part, mate_recv.at[plane]).start()
 
     for step in range(1, planes - 1):
@@ -422,7 +427,9 @@
                 aid_multiply(beside, h)
                 aid_across_got(h)
                 aid_multiply(across, h)
-            flags_up(mate).wait_recv()
+            for t in range(tiles):
+                stored = blocks[end_row, t, 0, pl.ds(0, 1)].astype(jnp.float32) > 0
+                aid_flags[t] = jnp.where(stored, 1.0, 0.0)[0]
             send_sums(end_row, aid_acc, aid_flags)
 
     def outside():
@@ -445,16 +452,29 @@
                 from_own(plane * CORES + c)
 
         def farthest(up, plane):
-            for h in range(SPLIT):
-                for c in range(CORES):
-                    k = plane * CORES + c
+            parts = [(h, c) for h in range(SPLIT) for c in range(CORES)]
+            for h, c in parts:
+                k = plane * CORES + c
+                if (h, c) == parts[-1]:
+                    got(last_body(k, core), recv.at[k if up else k - CORES, h])
+                    to_mate(last_body(k, core), late(plane, h, c), aid_send.at[1]).start()
+                    got(last_rest(k, core), last_sem.at[0])
+                else:
                     arrived(k, h, up)
-                    to_mate(blocks.at[k, core, h], late(plane, h)).start()
-                    multiply_piece(k, core, h)
-            for h in range(SPLIT):
-                got(blocks.at[pl.ds(plane * CORES, CORES), 1 - core, h], late(plane, h))
-                for c in range(CORES):
-                    multiply_piece(plane * CORES + c, 1 - core, h)
+                    sem = z_send if h == SPLIT - 1 else mate_send
+                    to_mate(blocks.at[k, core, h], late(plane, h, c), sem).start()
+                multiply_piece(k, core, h)
+            for h, c in parts:
+                k = plane * CORES + c
+                if (h, c) == parts[-1]:
+                    got(last_rest(k, 1 - core), last_sem.at[1])
+                    got(last_body(k, 1 - core), late(plane, h, c))
+                elif h:
+                    got(blocks.at[k, 1 - core, h], late(plane, h, c))
+                elif c == 0:
+                    both = blocks.at[pl.ds(plane * CORES, CORES), 1 - core, h]
+                    got(both, late(plane, h, c))
+                multiply_piece(k, 1 - core, h)
 
         for distance in range(1, planes):
             body = nearer if distance < top else farthest
@@ -498,25 +518,21 @@
     def sent(part, sem):
         remote(part, part, sem, sem, mate).wait_send()
 
-    for p in range(planes):
-
-        @pl.when(z == p)
-        def _():
-            if p < top:
-                sent(blocks.at[pl.ds(0, (p + 1) * CORES), 0], z_send.at[0])
-            if p > 0:
-                sent(blocks.at[pl.ds(0, (planes - p) * CORES), 0], z_send.at[1])
-
-    sent(blocks.at[:, 0], mate_send)
+    @pl.when(is_inside)
+    def _():
+        sent(blocks.at[pl.ds(0, planes + 1)], z_send)
+        sent(blocks.at[:, 0], mate_send)
+
     sent(left.at[pl.ds(0, ncol - 1)], left_send)
 
     @pl.when(is_end)
     def _():
         if across:
             sent(blocks.at[pl.ds(0, len(across) * tiles), 0], aid_send.at[0])
-        if topped:
-            sent(by_top, aid_send.at[1])
-        flags_up(mate).wait_send()
+        number = len(beside) * topped + 1
+        sent(aid.at[pl.ds(0, number), 0, 0, pl.ds(kept, depth - kept)], aid_send.at[1])
+        sent(blocks.at[pl.ds(0, tiles * SPLIT + CORES - 1), 0, 0], z_send)
+        sent(blocks.at[pl.ds(0, nrow - 1), 0], mate_send)
 
     @pl.when(is_inside)
     def _():
@@ -525,9 +541,10 @@
     @pl.when(is_aide)
     def _():
         some_sums(nrow - 1).wait_send()
+        number = len(beside) * topped + 1
+        sent(aid.at[pl.ds(0, number), 0, 0, pl.ds(0, kept)], aid_send.at[1])
         if topped:
             sent(blocks.at[pl.ds(0, 3 * len(along_x)), 0], aid_send.at[0])
-            sent(not_by_top, aid_send.at[2])
         else:
             sent(blocks.at[pl.ds(0, len(beside) * CORES), 0], aid_send.at[0])
 
@@ -552,15 +569,14 @@
             pltpu.VMEM((tiles, width), jnp.float32),
             pltpu.VMEM((tiles, width), jnp.float32),
             pltpu.VMEM((nrow, tiles, width), jnp.float32),
-            dma((2,)),
-            dma((2,)),
+            dma,
             dma,
             dma((nrow - CORES, SPLIT)),
-            dma((nrow // CORES + SPLIT - 1,)),
+            dma((nrow // CORES + (SPLIT - 1) * CORES,)),
             dma,
             dma((2 * SPLIT + 1,)),
-            dma((3,)),
-            dma((2 * SPLIT + 2,)),
+            dma((2,)),
+            dma((2 * SPLIT,)),
             dma((2,)),
             dma((2,)),
         ],

time: 24.9 us -> 24.8 us (level)
  no operation moved by 1% of the time
where the time goes in v5:
time: 24.8 us; the launch traced here: 24.6 us
  Pallas kernels  23.8 us (96%)
  local copies, waits for them, and re-layouts  0.8 us (3%)
    pallas_call x1, Pallas kernels, on_device(): pl.pallas_call(functools.partial(kernel, nrow, ncol), out_shape=jax.Shape...  23.8 us
    unnamed x1, local copies, waits for them, and re-layouts  0.8 us

profile of v5, /device:TPU:0, one launch (start us, length us, event | category | flops | bytes accessed | tf_op | source)
XLA Modules:
  0.0 24.6 jit_solution(1639100608489914536)
XLA Ops:
  0.0 23.8 %cluster_step.1 = f32[1,2,256,256]{3,2,1,0:T(8,128)S(1)} custom-call(s32[1,2]{1,0:T(1,128)} %cols_hbm.1, bf16[1,2,256,256]{3,2,1,0:T(8,128)(2,1)} %flow_hbm.1), custom_call_target="tpu_custom_call" | custom-call | tf_op jit(solution)/shard_map/cluster_step/pallas_call | solution.py:556
  23.9 0.8 %copy.4 = f32[1,2,256,256]{3,2,1,0:T(8,128)} copy(f32[1,2,256,256]{3,2,1,0:T(8,128)S(1)} %cluster_step.1) | data formatting | bytes 1048576

commit v6 on v5

--- a/solution.py
+++ b/solution.py
@@ -175,7 +175,7 @@
 
     def aid_up(d, t, h):
         part = left.at[at(*d), t, h]
-        arrival = aid_recv.at[SPLIT + h]
+        arrival = aid_recv.at[h]
         return remote(part, aid.at[at(*d), t, h], aid_send.at[0], arrival, (inner_row, col))
 
     def top_up():
@@ -205,12 +205,8 @@
                 else:
                     send(h, c, beside)
 
-    def aid_beside_got(h):
-        got(aid.at[pl.ds(0, len(beside)), :, 0], aid_recv.at[h])
-
-    def aid_across_got(h):
-        if across:
-            got(aid.at[pl.ds(0, len(across)), :, 0], aid_recv.at[SPLIT + h])
+    def aid_got(h):
+        got(aid.at[pl.ds(0, ncol - 1), :, 0], aid_recv.at[h])
 
     own_to_mate = remote(left.at[col], blocks.at[row], mate_send, mate_recv.at[z], mate)
 
@@ -408,11 +404,8 @@
         def _():
             aid_own()
             for h in range(SPLIT // 2):
-                aid_beside_got(h)
-                aid_multiply(beside, h)
-            for h in range(SPLIT // 2):
-                aid_across_got(h)
-                aid_multiply(across, h)
+                aid_got(h)
+                aid_multiply(beside + across, h)
 
         if across:
             for h in range(SPLIT):
@@ -423,10 +416,8 @@
         @pl.when(is_aide)
         def _():
             for h in range(SPLIT // 2, SPLIT):
-                aid_beside_got(h)
-                aid_multiply(beside, h)
-                aid_across_got(h)
-                aid_multiply(across, h)
+                aid_got(h)
+                aid_multiply(beside + across, h)
             for t in range(tiles):
                 stored = blocks[end_row, t, 0, pl.ds(0, 1)].astype(jnp.float32) > 0
                 aid_flags[t] = jnp.where(stored, 1.0, 0.0)[0]
@@ -576,7 +567,7 @@
             dma,
             dma((2 * SPLIT + 1,)),
             dma((2,)),
-            dma((2 * SPLIT,)),
+            dma((SPLIT,)),
             dma((2,)),
             dma((2,)),
         ],

time: 24.8 us -> 24.8 us (level)
  no operation moved by 1% of the time
where the time goes in v6:
time: 24.8 us; the launch traced here: 24.7 us
  Pallas kernels  23.9 us (96%)
  local copies, waits for them, and re-layouts  0.8 us (3%)
    pallas_call x1, Pallas kernels, on_device(): pl.pallas_call(functools.partial(kernel, nrow, ncol), out_shape=jax.Shape...  23.9 us
    unnamed x1, local copies, waits for them, and re-layouts  0.8 us

profile of v6, /device:TPU:0, one launch (start us, length us, event | category | flops | bytes accessed | tf_op | source)
XLA Modules:
  0.0 24.7 jit_solution(6261999064269838290)
XLA Ops:
  0.0 23.9 %cluster_step.1 = f32[1,2,256,256]{3,2,1,0:T(8,128)S(1)} custom-call(s32[1,2]{1,0:T(1,128)} %cols_hbm.1, bf16[1,2,256,256]{3,2,1,0:T(8,128)(2,1)} %flow_hbm.1), custom_call_target="tpu_custom_call" | custom-call | tf_op jit(solution)/shard_map/cluster_step/pallas_call | solution.py:547
  23.9 0.8 %copy.4 = f32[1,2,256,256]{3,2,1,0:T(8,128)} copy(f32[1,2,256,256]{3,2,1,0:T(8,128)S(1)} %cluster_step.1) | data formatting | bytes 1048576

commit v7 on v5

--- a/solution.py
+++ b/solution.py
@@ -329,7 +329,7 @@
                     number = SPLIT * CORES - (h * CORES + c)
                     for _ in range(-(-len(fillers) // number)):
                         pl.when(is_inside)(fillers.pop(0))
-                for sign in (-1, 1):
+                for sign in (1, -1):
                     plane = z + sign * step
 
                     @pl.when(is_inside & (plane >= 0) & (plane < planes))

time: 24.8 us -> 24.8 us (level)
  no operation moved by 1% of the time
where the time goes in v7:
time: 24.8 us; the launch traced here: 24.7 us
  Pallas kernels  23.9 us (96%)
  local copies, waits for them, and re-layouts  0.8 us (3%)
    pallas_call x1, Pallas kernels, on_device(): pl.pallas_call(functools.partial(kernel, nrow, ncol), out_shape=jax.Shape...  23.9 us
    unnamed x1, local copies, waits for them, and re-layouts  0.8 us

profile of v7, /device:TPU:0, one launch (start us, length us, event | category | flops | bytes accessed | tf_op | source)
XLA Modules:
  0.0 24.7 jit_solution(7523346406896972574)
XLA Ops:
  0.0 23.9 %cluster_step.1 = f32[1,2,256,256]{3,2,1,0:T(8,128)S(1)} custom-call(s32[1,2]{1,0:T(1,128)} %cols_hbm.1, bf16[1,2,256,256]{3,2,1,0:T(8,128)(2,1)} %flow_hbm.1), custom_call_target="tpu_custom_call" | custom-call | tf_op jit(solution)/shard_map/cluster_step/pallas_call | solution.py:556
  23.9 0.8 %copy.4 = f32[1,2,256,256]{3,2,1,0:T(8,128)} copy(f32[1,2,256,256]{3,2,1,0:T(8,128)S(1)} %cluster_step.1) | data formatting | bytes 1048576
